TPU v7x, 32 devices: a whole 2x2x4 slice. The times are simulated.
32 devices in a mesh: blk: 16 (over z, y, core), tensor: 2 (over x).
Axes of the slice: x: 2, y: 2, z: 4, core: 2. Of those that a mesh axis runs over, the one named last changes fastest.
Arguments:
- tokens: bfloat16 [64, 8192], P('blk'), may hold values from -6 to 6
- gate_weight: bfloat16 [29568, 8192], P(('blk', 'tensor')), may hold values from -0.0625 to 0.0625
- up_weight: bfloat16 [29568, 8192], P(('blk', 'tensor')), may hold values from -0.0625 to 0.0625
- down_weight: bfloat16 [29568, 8192], P(('blk', 'tensor')), may hold values from -0.03125 to 0.03125
Outputs:
- mixed: bfloat16 [64, 8192], P(('blk', 'tensor'))
All inputs are finite; a program needn't handle non-finite values.
Results may differ from a plain program's by a relative error of at most 0.009.
Values may be sent and summed in bfloat16 or wider, within the bound.
A program may use at most 128 MiB of HBM per device.

v0:
```python
import jax
import jax.numpy as jnp
from jax import lax
from jax.sharding import PartitionSpec as P


def project_rows(left, weight):
    return lax.dot_general(
        left, weight, (((1,), (1,)), ((), ())), preferred_element_type=jnp.float32
    )


def per_device(tokens, gate_weight, up_weight, down_weight):
    piece = lax.all_gather(tokens, "blk", axis=0, tiled=True)
    gate = project_rows(piece, gate_weight)
    up_part = project_rows(piece, up_weight)
    hidden = (jax.nn.silu(gate) * up_part).astype(jnp.bfloat16)
    total = lax.psum_scatter(
        jnp.dot(hidden, down_weight, preferred_element_type=jnp.float32),
        ("blk", "tensor"),
        scatter_dimension=0,
        tiled=True,
    )
    return total.astype(jnp.bfloat16)


def solution(mesh):
    placed = (
        P("blk", None),
        P(("blk", "tensor"), None),
        P(("blk", "tensor"), None),
        P(("blk", "tensor"), None),
    )
    return jax.shard_map(
        per_device,
        mesh=mesh,
        in_specs=placed,
        out_specs=P(("blk", "tensor"), None),
        check_vma=False,
    )
```

profile of v0, /device:TPU:0, one launch (start us, length us, event | category | flops | bytes accessed | tf_op | source)
XLA Modules:
  0.0 145.2 jit_solution(6302948357680619052)
XLA Ops:
  6.5 0.0 all-gather.3.cloned.1.call-start
  6.5 0.7 all-gather.3.cloned.1.call-update
  7.3 42.9 %all-gather.3.cloned.1.call-done = bf16[16,4,8192]{2,1,0:T(4,128)(2,1)} async-done(((bf16[1,4,8192]{2,1,0:T(4,128)(2,1)}), bf16[16,4,8192]{2,1,0:T(4,128)(2,1)}) %all-gather.3.cloned.1.call-update) | async-done | bytes 1048592 | tf_op jit(solution)/shard_map/all_gather | solution.py:14
  50.1 1.3 reshape.1
  51.5 9.9 %fusion.9 = f32[64,924]{1,0:T(8,128)S(1)} fusion(bf16[64,8192]{1,0:T(8,128)(2,1)S(1)} %reshape.1, bf16[924,8192]{1,0:T(8,128)(2,1)} %param.5), kind=kOutput, calls=%fused_computation.11 | convolution fusion | flops 968884224 | bytes 16423936 | tf_op jit(solution)/shard_map/dot_general | solution.py:8
  61.4 14.4 %fusion.1 = f32[64,8192]{1,0:T(8,128)S(1)} fusion(bf16[924,8192]{1,0:T(8,128)(2,1)} %param.7, bf16[64,8192]{1,0:T(8,128)(2,1)S(1)} %reshape.1, bf16[924,8192]{1,0:T(8,128)(2,1)} %param.6, f32[64,924]{1,0:T(8,128)S(1)} %fusion.9), kind=kOutput, calls=%fused_computation.2 | convolution fusion | flops 1938123264 | bytes 33659904 | tf_op jit(solution)/shard_map/dot_general | solution.py:19
  75.8 61.9 %all-reduce.2 = bf16[64,8192]{1,0:T(8,128)(2,1)S(1)} all-reduce(f32[64,8192]{1,0:T(8,128)S(1)} %fusion.1), channel_id=2, replica_groups=mesh['blk'=16,'tensor'=2] {'blk','tensor'}, use_global_device_ids=true, to_apply=%region_0.1.clone | all-reduce | flops 524288 | bytes 3145728
  137.7 0.7 dynamic-slice_convert_fusion
Async XLA Ops:
  6.5 43.6 %all-gather.3.cloned.1.call-start = ((), (), s32[]{:S(2)}) async-start(), calls=%async_computation | async-start | bytes 1114112 | tf_op jit(solution)/shard_map/all_gather | solution.py:14
Sparse Core Ops, SparseCore 0:
  9.5 40.5 all-gather.2
where the time goes:
time: 145 us
  blocking collectives  61.9 us (43%)
  waiting for transfers between devices  43.6 us (30%)
  matrix products  24.3 us (17%)
  between operations  13.4 us (9%)
  local copies, waits for them, and re-layouts  1.99 us (1%)
    unnamed x1, blocking collectives  61.9 us
    all_gather x1, waiting for transfers between devices, per_device(): piece = lax.all_gather(tokens, 'blk', axis=0, tiled=True)  42.9 us
    dot_general x1, matrix products, per_device(): jnp.dot(hidden, down_weight, preferred_element_type=jnp.float32)  14.4 us
    dot_general x1, matrix products, project_rows(): lax.dot_general(left, weight, (((1,), (1,)), ((), ())), preferred_element...  9.94 us
  transfers between devices with their start and end apart: 1, of which 1 were waited for; matrix products, arithmetic and copies ran while one was open for 0% of the time, Pallas kernels for 0%

commit v1 on v0

--- a/solution.py
+++ b/solution.py
@@ -11,7 +11,12 @@
 
 
 def per_device(tokens, gate_weight, up_weight, down_weight):
-    piece = lax.all_gather(tokens, "blk", axis=0, tiled=True)
+    ring = [tokens]
+    for hop in range(15):
+        ring.append(lax.ppermute(ring[-1], "blk", [(dev, (dev + 1) % 16) for dev in range(16)]))
+    piece = jnp.roll(
+        jnp.concatenate(ring[::-1], axis=0), (lax.axis_index("blk") + 1) * ring[0].shape[0], axis=0
+    )
     gate = project_rows(piece, gate_weight)
     up_part = project_rows(piece, up_weight)
     hidden = (jax.nn.silu(gate) * up_part).astype(jnp.bfloat16)

time: 145 us -> 190 us (1.31)
  waiting for transfers between devices: 43.6 us -> 96.5 us
  between operations: 13.4 us -> 0.04 us
  matrix products: 24.3 us -> 28.1 us
  local copies, waits for them, and re-layouts: 1.99 us -> 4.19 us
    ppermute x0 -> x15, waiting for transfers between devices: none -> 96.5 us  [per_device(): lax.ppermute(ring[-1], 'blk', [(dev, (dev + 1) % 16) for dev in range(16)])]
    all_gather x1 -> x0, waiting for transfers between devices: 42.9 us -> none  [per_device(): piece = lax.all_gather(tokens, 'blk', axis=0, tiled=True)]
    dot_general x1 -> x2, matrix products: 9.94 us -> 19.9 us  [project_rows(): lax.dot_general(left, weight, (((1,), (1,)), ((), ())), preferred_element...]
    dot_general x1, matrix products: 14.4 us -> 8.12 us  [per_device(): jnp.dot(hidden, down_weight, preferred_element_type=jnp.float32)]
    concatenate x0 -> x1, local copies, waits for them, and re-layouts: none -> 3.53 us  [per_device(): jnp.roll(jnp.concatenate(ring[::-1], axis=0), (lax.axis_index('blk') + 1)...]
  transfers between devices with their start and end apart: 1 -> 15, of which waited for: 1 -> 15; matrix products, arithmetic and copies ran while one was open for 0% -> 0% of each run, Pallas kernels for 0% -> 0%
where the time goes in v1:
time: 190 us
  waiting for transfers between devices  96.5 us (51%)
  blocking collectives  60.5 us (32%)
  matrix products  28.1 us (15%)
  local copies, waits for them, and re-layouts  4.19 us (2%)
    ppermute x15, waiting for transfers between devices, per_device(): lax.ppermute(ring[-1], 'blk', [(dev, (dev + 1) % 16) for dev in range(16)])  96.5 us
    unnamed x1, blocking collectives  60.5 us
    dot_general x2, matrix products, project_rows(): lax.dot_general(left, weight, (((1,), (1,)), ((), ())), preferred_element...  19.9 us
    dot_general x1, matrix products, per_device(): jnp.dot(hidden, down_weight, preferred_element_type=jnp.float32)  8.12 us
  transfers between devices with their start and end apart: 15, of which 15 were waited for; matrix products, arithmetic and copies ran while one was open for 0% of the time, Pallas kernels for 0%

profile of v1, /device:TPU:0, one launch (start us, length us, event | category | flops | bytes accessed | tf_op | source)
XLA Modules:
  0.0 189.8 jit_solution(10782770450845262784)
XLA Ops:
  0.0 0.5 collective-permute-start
  0.5 7.1 %collective-permute-done = bf16[4,8192]{1,0:T(4,128)(2,1)S(1)} collective-permute-done((bf16[4,8192]{1,0:T(4,128)(2,1)}, bf16[4,8192]{1,0:T(4,128)(2,1)S(1)}, u32[]{:S(2)}, u32[]{:S(2)}) %collective-permute-start) | collective-permute-done | bytes 65568 | tf_op jit(solution)/shard_map/ppermute | solution.py:16
  7.6 0.0 collective-permute-start.1
  7.6 6.4 %collective-permute-done.1 = bf16[4,8192]{1,0:T(4,128)(2,1)S(1)} collective-permute-done((bf16[4,8192]{1,0:T(4,128)(2,1)S(1)}, bf16[4,8192]{1,0:T(4,128)(2,1)S(1)}, u32[]{:S(2)}, u32[]{:S(2)}) %collective-permute-start.1) | collective-permute-done | bytes 65568 | tf_op jit(solution)/shard_map/ppermute | solution.py:16
  14.0 0.0 collective-permute-start.2
  14.0 6.4 %collective-permute-done.2 = bf16[4,8192]{1,0:T(4,128)(2,1)S(1)} collective-permute-done((bf16[4,8192]{1,0:T(4,128)(2,1)S(1)}, bf16[4,8192]{1,0:T(4,128)(2,1)S(1)}, u32[]{:S(2)}, u32[]{:S(2)}) %collective-permute-start.2) | collective-permute-done | bytes 65568 | tf_op jit(solution)/shard_map/ppermute | solution.py:16
  20.4 0.0 collective-permute-start.3
  20.4 6.4 %collective-permute-done.3 = bf16[4,8192]{1,0:T(4,128)(2,1)S(1)} collective-permute-done((bf16[4,8192]{1,0:T(4,128)(2,1)S(1)}, bf16[4,8192]{1,0:T(4,128)(2,1)S(1)}, u32[]{:S(2)}, u32[]{:S(2)}) %collective-permute-start.3) | collective-permute-done | bytes 65568 | tf_op jit(solution)/shard_map/ppermute | solution.py:16
  26.8 0.0 collective-permute-start.4
  26.8 6.4 %collective-permute-done.4 = bf16[4,8192]{1,0:T(4,128)(2,1)S(1)} collective-permute-done((bf16[4,8192]{1,0:T(4,128)(2,1)S(1)}, bf16[4,8192]{1,0:T(4,128)(2,1)S(1)}, u32[]{:S(2)}, u32[]{:S(2)}) %collective-permute-start.4) | collective-permute-done | bytes 65568 | tf_op jit(solution)/shard_map/ppermute | solution.py:16
  33.2 0.0 collective-permute-start.5
  33.2 6.4 %collective-permute-done.5 = bf16[4,8192]{1,0:T(4,128)(2,1)S(1)} collective-permute-done((bf16[4,8192]{1,0:T(4,128)(2,1)S(1)}, bf16[4,8192]{1,0:T(4,128)(2,1)S(1)}, u32[]{:S(2)}, u32[]{:S(2)}) %collective-permute-start.5) | collective-permute-done | bytes 65568 | tf_op jit(solution)/shard_map/ppermute | solution.py:16
  39.6 0.0 collective-permute-start.6
  39.6 6.4 %collective-permute-done.6 = bf16[4,8192]{1,0:T(4,128)(2,1)S(1)} collective-permute-done((bf16[4,8192]{1,0:T(4,128)(2,1)S(1)}, bf16[4,8192]{1,0:T(4,128)(2,1)S(1)}, u32[]{:S(2)}, u32[]{:S(2)}) %collective-permute-start.6) | collective-permute-done | bytes 65568 | tf_op jit(solution)/shard_map/ppermute | solution.py:16
  46.0 0.0 collective-permute-start.7
  46.0 6.4 %collective-permute-done.7 = bf16[4,8192]{1,0:T(4,128)(2,1)S(1)} collective-permute-done((bf16[4,8192]{1,0:T(4,128)(2,1)S(1)}, bf16[4,8192]{1,0:T(4,128)(2,1)S(1)}, u32[]{:S(2)}, u32[]{:S(2)}) %collective-permute-start.7) | collective-permute-done | bytes 65568 | tf_op jit(solution)/shard_map/ppermute | solution.py:16
  52.4 0.0 collective-permute-start.8
  52.4 6.4 %collective-permute-done.8 = bf16[4,8192]{1,0:T(4,128)(2,1)S(1)} collective-permute-done((bf16[4,8192]{1,0:T(4,128)(2,1)S(1)}, bf16[4,8192]{1,0:T(4,128)(2,1)S(1)}, u32[]{:S(2)}, u32[]{:S(2)}) %collective-permute-start.8) | collective-permute-done | bytes 65568 | tf_op jit(solution)/shard_map/ppermute | solution.py:16
  58.7 0.0 collective-permute-start.9
  58.7 6.4 %collective-permute-done.9 = bf16[4,8192]{1,0:T(4,128)(2,1)S(1)} collective-permute-done((bf16[4,8192]{1,0:T(4,128)(2,1)S(1)}, bf16[4,8192]{1,0:T(4,128)(2,1)S(1)}, u32[]{:S(2)}, u32[]{:S(2)}) %collective-permute-start.9) | collective-permute-done | bytes 65568 | tf_op jit(solution)/shard_map/ppermute | solution.py:16
  65.1 0.0 collective-permute-start.10
  65.1 6.4 %collective-permute-done.10 = bf16[4,8192]{1,0:T(4,128)(2,1)S(1)} collective-permute-done((bf16[4,8192]{1,0:T(4,128)(2,1)S(1)}, bf16[4,8192]{1,0:T(4,128)(2,1)S(1)}, u32[]{:S(2)}, u32[]{:S(2)}) %collective-permute-start.10) | collective-permute-done | bytes 65568 | tf_op jit(solution)/shard_map/ppermute | solution.py:16
  71.5 0.0 collective-permute-start.11
  71.5 6.4 %collective-permute-done.11 = bf16[4,8192]{1,0:T(4,128)(2,1)S(1)} collective-permute-done((bf16[4,8192]{1,0:T(4,128)(2,1)S(1)}, bf16[4,8192]{1,0:T(4,128)(2,1)S(1)}, u32[]{:S(2)}, u32[]{:S(2)}) %collective-permute-start.11) | collective-permute-done | bytes 65568 | tf_op jit(solution)/shard_map/ppermute | solution.py:16
  77.9 0.0 collective-permute-start.12
  77.9 6.4 %collective-permute-done.12 = bf16[4,8192]{1,0:T(4,128)(2,1)S(1)} collective-permute-done((bf16[4,8192]{1,0:T(4,128)(2,1)S(1)}, bf16[4,8192]{1,0:T(4,128)(2,1)S(1)}, u32[]{:S(2)}, u32[]{:S(2)}) %collective-permute-start.12) | collective-permute-done | bytes 65568 | tf_op jit(solution)/shard_map/ppermute | solution.py:16
  84.3 0.0 collective-permute-start.13
  84.3 6.4 %collective-permute-done.13 = bf16[4,8192]{1,0:T(4,128)(2,1)S(1)} collective-permute-done((bf16[4,8192]{1,0:T(4,128)(2,1)S(1)}, bf16[4,8192]{1,0:T(4,128)(2,1)S(1)}, u32[]{:S(2)}, u32[]{:S(2)}) %collective-permute-start.13) | collective-permute-done | bytes 65568 | tf_op jit(solution)/shard_map/ppermute | solution.py:16
  90.7 0.0 collective-permute-start.14
  90.7 6.4 %collective-permute-done.14 = bf16[4,8192]{1,0:T(4,128)(2,1)S(1)} collective-permute-done((bf16[4,8192]{1,0:T(4,128)(2,1)S(1)}, bf16[4,8192]{1,0:T(4,128)(2,1)S(1)}, u32[]{:S(2)}, u32[]{:S(2)}) %collective-permute-start.14) | collective-permute-done | bytes 65568 | tf_op jit(solution)/shard_map/ppermute | solution.py:16
  97.1 3.5 %concatenate.6 = bf16[128,8192]{1,0:T(8,128)(2,1)S(1)} concatenate(bf16[4,8192]{1,0:T(4,128)(2,1)S(1)} %collective-permute-done.14, bf16[4,8192]{1,0:T(4,128)(2,1)S(1)} %collective-permute-done.13, bf16[4,8192]{1,0:T(4,128)(2,1)S(1)} %collective-permute-done.12, bf16[4,8192]{1,0:T(4,128)(2,1)S(1)} %collective-permute-done.11, bf16[4,8192]{1,0:T(4,128)(2,1)S(1)} %collective-permute-done.10, ...), dimensions={0} | concatenate | bytes 4194304 | tf_op jit(solution)/shard_map/jit(_roll_dynamic)/concatenate | solution.py:17
  100.6 10.0 %fusion.2 = f32[64,924]{1,0:T(8,128)S(1)} fusion(bf16[924,8192]{1,0:T(8,128)(2,1)} %param.5, bf16[128,8192]{1,0:T(8,128)(2,1)S(1)} %concatenate.6, s32[]{:T(128)S(6)} %select_n.14), kind=kOutput, calls=%fused_computation.2 | convolution fusion | flops 968884224 | bytes 16423940 | tf_op jit(solution)/shard_map/dot_general | solution.py:8
  110.6 10.0 %fusion = f32[64,924]{1,0:T(8,128)S(1)} fusion(bf16[924,8192]{1,0:T(8,128)(2,1)} %param.6, bf16[128,8192]{1,0:T(8,128)(2,1)S(1)} %concatenate.6, s32[]{:T(128)S(6)} %select_n.14), kind=kOutput, calls=%fused_computation | convolution fusion | flops 968884224 | bytes 16423940 | tf_op jit(solution)/shard_map/dot_general | solution.py:8
  120.5 8.1 %fusion.4 = f32[64,8192]{1,0:T(8,128)S(1)} fusion(bf16[924,8192]{1,0:T(8,128)(2,1)} %param.7, f32[64,924]{1,0:T(8,128)S(1)} %fusion, f32[64,924]{1,0:T(8,128)S(1)} %fusion.2), kind=kOutput, calls=%fused_computation.5 | convolution fusion | flops 969239040 | bytes 17709056 | tf_op jit(solution)/shard_map/dot_general | solution.py:24
  128.7 60.5 %all-reduce.2 = bf16[64,8192]{1,0:T(8,128)(2,1)S(1)} all-reduce(f32[64,8192]{1,0:T(8,128)S(1)} %fusion.4), channel_id=2, replica_groups=mesh['blk'=16,'tensor'=2] {'blk','tensor'}, use_global_device_ids=true, to_apply=%region_0.1.clone | all-reduce | flops 524288 | bytes 3145728
  189.2 0.7 dynamic-slice_convert_fusion
Async XLA Ops:
  0.0 7.6 %collective-permute-start = (bf16[4,8192]{1,0:T(4,128)(2,1)}, bf16[4,8192]{1,0:T(4,128)(2,1)S(1)}, u32[]{:S(2)}, u32[]{:S(2)}) collective-permute-start(bf16[4,8192]{1,0:T(4,128)(2,1)} %param.4), channel_id=1, source_target_pairs={{0,2},{2,4},{4,6},{6,8},{8,10},{10,12},{12,14},{14,16},{16,18},{18... | collective-permute-start | bytes 196616 | tf_op jit(solution)/shard_map/ppermute | solution.py:16
  7.6 6.4 %collective-permute-start.1 = (bf16[4,8192]{1,0:T(4,128)(2,1)S(1)}, bf16[4,8192]{1,0:T(4,128)(2,1)S(1)}, u32[]{:S(2)}, u32[]{:S(2)}) collective-permute-start(bf16[4,8192]{1,0:T(4,128)(2,1)S(1)} %collective-permute-done), channel_id=1, source_target_pairs={{0,2},{2,4},{4,6},{6,8},{8,10},{10,12},{12,14},{14,16},{16,18},{18... | collective-permute-start | bytes 196616 | tf_op jit(solution)/shard_map/ppermute | solution.py:16
  14.0 6.4 %collective-permute-start.2 = (bf16[4,8192]{1,0:T(4,128)(2,1)S(1)}, bf16[4,8192]{1,0:T(4,128)(2,1)S(1)}, u32[]{:S(2)}, u32[]{:S(2)}) collective-permute-start(bf16[4,8192]{1,0:T(4,128)(2,1)S(1)} %collective-permute-done.1), channel_id=1, source_target_pairs={{0,2},{2,4},{4,6},{6,8},{8,10},{10,12},{12,14},{14,16},{16,18},{18... | collective-permute-start | bytes 196616 | tf_op jit(solution)/shard_map/ppermute | solution.py:16
  20.4 6.4 %collective-permute-start.3 = (bf16[4,8192]{1,0:T(4,128)(2,1)S(1)}, bf16[4,8192]{1,0:T(4,128)(2,1)S(1)}, u32[]{:S(2)}, u32[]{:S(2)}) collective-permute-start(bf16[4,8192]{1,0:T(4,128)(2,1)S(1)} %collective-permute-done.2), channel_id=1, source_target_pairs={{0,2},{2,4},{4,6},{6,8},{8,10},{10,12},{12,14},{14,16},{16,18},{18... | collective-permute-start | bytes 196616 | tf_op jit(solution)/shard_map/ppermute | solution.py:16
  26.8 6.4 %collective-permute-start.4 = (bf16[4,8192]{1,0:T(4,128)(2,1)S(1)}, bf16[4,8192]{1,0:T(4,128)(2,1)S(1)}, u32[]{:S(2)}, u32[]{:S(2)}) collective-permute-start(bf16[4,8192]{1,0:T(4,128)(2,1)S(1)} %collective-permute-done.3), channel_id=1, source_target_pairs={{0,2},{2,4},{4,6},{6,8},{8,10},{10,12},{12,14},{14,16},{16,18},{18... | collective-permute-start | bytes 196616 | tf_op jit(solution)/shard_map/ppermute | solution.py:16
  33.2 6.4 %collective-permute-start.5 = (bf16[4,8192]{1,0:T(4,128)(2,1)S(1)}, bf16[4,8192]{1,0:T(4,128)(2,1)S(1)}, u32[]{:S(2)}, u32[]{:S(2)}) collective-permute-start(bf16[4,8192]{1,0:T(4,128)(2,1)S(1)} %collective-permute-done.4), channel_id=1, source_target_pairs={{0,2},{2,4},{4,6},{6,8},{8,10},{10,12},{12,14},{14,16},{16,18},{18... | collective-permute-start | bytes 196616 | tf_op jit(solution)/shard_map/ppermute | solution.py:16
  39.6 6.4 %collective-permute-start.6 = (bf16[4,8192]{1,0:T(4,128)(2,1)S(1)}, bf16[4,8192]{1,0:T(4,128)(2,1)S(1)}, u32[]{:S(2)}, u32[]{:S(2)}) collective-permute-start(bf16[4,8192]{1,0:T(4,128)(2,1)S(1)} %collective-permute-done.5), channel_id=1, source_target_pairs={{0,2},{2,4},{4,6},{6,8},{8,10},{10,12},{12,14},{14,16},{16,18},{18... | collective-permute-start | bytes 196616 | tf_op jit(solution)/shard_map/ppermute | solution.py:16
  46.0 6.4 %collective-permute-start.7 = (bf16[4,8192]{1,0:T(4,128)(2,1)S(1)}, bf16[4,8192]{1,0:T(4,128)(2,1)S(1)}, u32[]{:S(2)}, u32[]{:S(2)}) collective-permute-start(bf16[4,8192]{1,0:T(4,128)(2,1)S(1)} %collective-permute-done.6), channel_id=1, source_target_pairs={{0,2},{2,4},{4,6},{6,8},{8,10},{10,12},{12,14},{14,16},{16,18},{18... | collective-permute-start | bytes 196616 | tf_op jit(solution)/shard_map/ppermute | solution.py:16
  52.4 6.4 %collective-permute-start.8 = (bf16[4,8192]{1,0:T(4,128)(2,1)S(1)}, bf16[4,8192]{1,0:T(4,128)(2,1)S(1)}, u32[]{:S(2)}, u32[]{:S(2)}) collective-permute-start(bf16[4,8192]{1,0:T(4,128)(2,1)S(1)} %collective-permute-done.7), channel_id=1, source_target_pairs={{0,2},{2,4},{4,6},{6,8},{8,10},{10,12},{12,14},{14,16},{16,18},{18... | collective-permute-start | bytes 196616 | tf_op jit(solution)/shard_map/ppermute | solution.py:16
  58.7 6.4 %collective-permute-start.9 = (bf16[4,8192]{1,0:T(4,128)(2,1)S(1)}, bf16[4,8192]{1,0:T(4,128)(2,1)S(1)}, u32[]{:S(2)}, u32[]{:S(2)}) collective-permute-start(bf16[4,8192]{1,0:T(4,128)(2,1)S(1)} %collective-permute-done.8), channel_id=1, source_target_pairs={{0,2},{2,4},{4,6},{6,8},{8,10},{10,12},{12,14},{14,16},{16,18},{18... | collective-permute-start | bytes 196616 | tf_op jit(solution)/shard_map/ppermute | solution.py:16
  65.1 6.4 %collective-permute-start.10 = (bf16[4,8192]{1,0:T(4,128)(2,1)S(1)}, bf16[4,8192]{1,0:T(4,128)(2,1)S(1)}, u32[]{:S(2)}, u32[]{:S(2)}) collective-permute-start(bf16[4,8192]{1,0:T(4,128)(2,1)S(1)} %collective-permute-done.9), channel_id=1, source_target_pairs={{0,2},{2,4},{4,6},{6,8},{8,10},{10,12},{12,14},{14,16},{16,18},{18... | collective-permute-start | bytes 196616 | tf_op jit(solution)/shard_map/ppermute | solution.py:16
  71.5 6.4 %collective-permute-start.11 = (bf16[4,8192]{1,0:T(4,128)(2,1)S(1)}, bf16[4,8192]{1,0:T(4,128)(2,1)S(1)}, u32[]{:S(2)}, u32[]{:S(2)}) collective-permute-start(bf16[4,8192]{1,0:T(4,128)(2,1)S(1)} %collective-permute-done.10), channel_id=1, source_target_pairs={{0,2},{2,4},{4,6},{6,8},{8,10},{10,12},{12,14},{14,16},{16,18},{18... | collective-permute-start | bytes 196616 | tf_op jit(solution)/shard_map/ppermute | solution.py:16
  77.9 6.4 %collective-permute-start.12 = (bf16[4,8192]{1,0:T(4,128)(2,1)S(1)}, bf16[4,8192]{1,0:T(4,128)(2,1)S(1)}, u32[]{:S(2)}, u32[]{:S(2)}) collective-permute-start(bf16[4,8192]{1,0:T(4,128)(2,1)S(1)} %collective-permute-done.11), channel_id=1, source_target_pairs={{0,2},{2,4},{4,6},{6,8},{8,10},{10,12},{12,14},{14,16},{16,18},{18... | collective-permute-start | bytes 196616 | tf_op jit(solution)/shard_map/ppermute | solution.py:16
  84.3 6.4 %collective-permute-start.13 = (bf16[4,8192]{1,0:T(4,128)(2,1)S(1)}, bf16[4,8192]{1,0:T(4,128)(2,1)S(1)}, u32[]{:S(2)}, u32[]{:S(2)}) collective-permute-start(bf16[4,8192]{1,0:T(4,128)(2,1)S(1)} %collective-permute-done.12), channel_id=1, source_target_pairs={{0,2},{2,4},{4,6},{6,8},{8,10},{10,12},{12,14},{14,16},{16,18},{18... | collective-permute-start | bytes 196616 | tf_op jit(solution)/shard_map/ppermute | solution.py:16
  90.7 6.4 %collective-permute-start.14 = (bf16[4,8192]{1,0:T(4,128)(2,1)S(1)}, bf16[4,8192]{1,0:T(4,128)(2,1)S(1)}, u32[]{:S(2)}, u32[]{:S(2)}) collective-permute-start(bf16[4,8192]{1,0:T(4,128)(2,1)S(1)} %collective-permute-done.13), channel_id=1, source_target_pairs={{0,2},{2,4},{4,6},{6,8},{8,10},{10,12},{12,14},{14,16},{16,18},{18... | collective-permute-start | bytes 196616 | tf_op jit(solution)/shard_map/ppermute | solution.py:16
